TPU v7x, 16 devices: a 4x2x1 block of a 4x4x4 slice. The times are simulated.
16 devices in a mesh: dp: 4 (over y, z, core), sp: 4 (over x).
Axes of the slice: x: 4, y: 2, z: 1, core: 2. Of those that a mesh axis runs over, the one named last changes fastest.
The devices are a block of a 4x4x4 slice.
Arguments:
- q: bfloat16 [128, 40, 128], P('dp'), parts along dimension 0
- k: bfloat16 [128, 4096, 10, 128], P('dp', 'sp'), parts along dimension 0
- v: bfloat16 [128, 4096, 10, 128], P('dp', 'sp'), parts along dimension 0
Outputs:
- q: bfloat16 [128, 40, 128], P('dp'), parts along dimension 0
There are 4 independent parts. A program takes and returns all parts, laid end to end along the dimension named above; each array names one.
All inputs are finite; a program needn't handle non-finite values.
Results may differ from a plain program's by a relative error of at most 0.012.
Values are sent between devices in bfloat16 or wider.
A program may use at most 1.5 GiB of HBM per device.

v0:
```python
import jax
import jax.numpy as jnp
from jax import lax
from jax.sharding import PartitionSpec as P


def einsum(form, a, b):
    return jnp.einsum(form, a.astype(jnp.float32), b.astype(jnp.float32))


def part_of(q, k, v):
    grouped = q.reshape(q.shape[0], k.shape[2], -1, q.shape[2])
    scores = einsum("bgsd,bugd->bgsu", grouped, k) * q.shape[2] ** -0.5
    high = jnp.max(scores, -1, keepdims=True)
    weights = jnp.exp(scores - high)
    seen = einsum("bgsu,bugd->bgsd", weights.astype(jnp.bfloat16), v)
    return jnp.concatenate([seen, jnp.sum(weights, -1, keepdims=True), high], -1)


def together(parts):
    seen, total, high = parts[..., :-2], parts[..., -2:-1], parts[..., -1:]
    scale = jnp.exp(high - jnp.max(high, 0))
    return (jnp.sum(seen * scale, 0) / jnp.sum(total * scale, 0)).astype(jnp.bfloat16)


def solution(mesh):
    def step(q, k, v):
        return together(lax.all_gather(part_of(q, k, v), "sp")).reshape(q.shape)

    return jax.shard_map(
        step,
        mesh=mesh,
        in_specs=(P("dp", None, None), P("dp", "sp", None, None), P("dp", "sp", None, None)),
        out_specs=P("dp", None, None),
        check_vma=False,
    )
```

profile of v0, /device:TPU:112, one launch (start us, length us, event | category | flops | bytes accessed | tf_op | source)
XLA Modules:
  0.0 159.5 jit_solution(9648513279144395144)
XLA Ops:
  6.5 0.0 copy-start
  6.6 0.0 all-gather.3.cloned.1.call-start
  6.6 1.0 copy-done
  7.5 33.2 %multiply_reduce_fusion = (f32[32,10,4]{2,1,0:T(8,128)S(1)}, f32[32,10,4,1024]{3,2,1,0:T(4,128)}) fusion(bf16[32,10,4,128]{3,2,1,0:T(4,128)(2,1)S(1)} %bitcast.11, bf16[32,1024,10,128]{3,1,2,0:T(8,128)(2,1)} %param.4), kind=kOutput, calls=%fused_computation.1 | convolution fusion | flops 338164480 | bytes 89461760 | tf_op jit(solution)/shard_map/bgsd,bugd->bgsu/dot_general | solution.py:8
  40.7 5.3 %fusion = f32[32,10,4]{2,1,0:T(8,128)S(1)} fusion(f32[32,10,4,1024]{3,2,1,0:T(4,128)} %get-tuple-element.11, f32[32,10,4]{2,1,0:T(8,128)S(1)} %get-tuple-element.10), kind=kLoop, calls=%fused_computation.2 | loop fusion | flops 3930880 | bytes 5253120 | tf_op jit(solution)/shard_map/reduce_sum | solution.py:17
  46.0 29.9 %fusion.2 = f32[32,10,4,128]{3,2,1,0:T(4,128)S(1)} fusion(bf16[32,1024,10,128]{3,1,2,0:T(8,128)(2,1)} %param.5, f32[32,10,4,1024]{3,2,1,0:T(4,128)} %get-tuple-element.11, f32[32,10,4]{2,1,0:T(8,128)S(1)} %get-tuple-element.10), kind=kOutput, calls=%fused_computation.4 | convolution fusion | flops 339476480 | bytes 89789440 | tf_op jit(solution)/shard_map/bgsu,bugd->bgsd/dot_general | solution.py:8
  75.9 2.1 %copy.13 = f32[32,10,4,1]{3,2,1,0:T(4,128)S(1)} copy(f32[32,10,4,1]{2,1,0,3:T(8,128)S(1)} %bitcast.16) | data formatting | bytes 10240 | tf_op jit(solution)/shard_map/broadcast_in_dim | solution.py:17
  78.0 2.1 %copy.14 = f32[32,10,4,1]{3,2,1,0:T(4,128)S(1)} copy(f32[32,10,4,1]{2,1,0,3:T(8,128)S(1)} %bitcast.14) | data formatting | bytes 10240 | tf_op jit(solution)/shard_map/broadcast_in_dim | solution.py:14
  80.0 1.6 %pad_maximum_fusion = f32[32,10,4,130]{3,2,1,0:T(4,128)} fusion(f32[32,10,4,1]{3,2,1,0:T(4,128)S(1)} %copy.14, f32[32,10,4,1]{3,2,1,0:T(4,128)S(1)} %copy.13, f32[32,10,4,128]{3,2,1,0:T(4,128)S(1)} %fusion.2), kind=kLoop, calls=%fused_computation.9 | loop fusion | flops 332800 | bytes 1331200 | tf_op jit(solution)/shard_map/concatenate | solution.py:17
  81.6 0.1 all-gather.3.cloned.1.call-update
  81.7 55.8 %all-gather.3.cloned.1.call-done = f32[128,10,4,130]{3,2,1,0:T(4,128)} async-done(((f32[32,10,4,130]{3,2,1,0:T(4,128)}), f32[128,10,4,130]{3,2,1,0:T(4,128)}) %all-gather.3.cloned.1.call-update) | async-done | bytes 2662416 | tf_op jit(solution)/shard_map/all_gather | solution.py:28
  137.5 6.0 %fusion.9 = (f32[4,32,10,4,1]{4,3,2,1,0:T(4,128)}, f32[32,10,4]{2,1,0:T(8,128)S(1)}, f32[4,32,10,4,1]{4,3,2,1,0:T(4,128)S(1)}) fusion(f32[4,32,10,4,130]{4,3,2,1,0:T(4,128)} %bitcast.12), kind=kLoop, calls=%fused_computation.16 | loop fusion | flops 3840 | bytes 87040 | tf_op jit(solution)/shard_map/slice | solution.py:21
  143.4 2.4 %copy.24 = f32[4,32,10,4,1]{1,3,2,0,4:T(4,128)S(1)} copy(f32[4,32,10,4,1]{4,3,2,1,0:T(4,128)} %get-tuple-element.5) | data formatting | bytes 40960
  145.9 0.1 copy.25
  146.0 1.3 copy.23
  147.3 0.1 multiply_reduce_fusion.1
  147.4 0.1 copy.18
  147.4 0.5 copy.16
  148.0 3.7 %fusion.4 = f32[32,10,4,128]{3,2,1,0:T(4,128)S(1)} fusion(f32[4,32,10,4,130]{4,3,2,1,0:T(4,128)} %bitcast.13, f32[4,32,10,4]{3,2,1,0:T(8,128)S(1)} %copy.16), kind=kLoop, calls=%fused_computation.6 | loop fusion | flops 1146880 | bytes 3297280 | tf_op jit(solution)/shard_map/reduce_sum | solution.py:23
  151.7 1.0 divide_convert_fusion
Async XLA Ops:
  6.5 1.0 copy-start
  6.6 130.9 %all-gather.3.cloned.1.call-start = ((), (), s32[]{:S(2)}) async-start(), calls=%async_computation | async-start | bytes 6553600 | tf_op jit(solution)/shard_map/all_gather | solution.py:28
Sparse Core Ops, SparseCore 0:
  81.8 55.6 all-gather.2
where the time goes:
time: 160 us; the launch traced here: 159 us
  matrix products  63.1 us (39%)
  waiting for transfers between devices  55.9 us (35%)
  other arithmetic  17.6 us (11%)
  between operations  13.4 us (8%)
  local copies, waits for them, and re-layouts  9.52 us (6%)
    dot_general x2, matrix products, einsum(): return jnp.einsum(form, a.astype(jnp.float32), b.astype(jnp.float32))  63.1 us
    all_gather x1, waiting for transfers between devices, step(): return together(lax.all_gather(part_of(q, k, v), 'sp')).reshape(q.shape)  55.8 us
    slice x1, other arithmetic, together(): seen, total, high = (parts[..., :-2], parts[..., -2:-1], parts[..., -1:])  5.95 us
    reduce_sum x1, other arithmetic, part_of(): jnp.sum(weights, -1, keepdims=True)  5.32 us
    unnamed x5, local copies, waits for them, and re-layouts  4.81 us
    reduce_sum x1, other arithmetic, together(): jnp.sum(seen * scale, 0) / jnp.sum(total * scale, 0)  3.69 us
  transfers between devices with their start and end apart: 1, of which 1 were waited for; matrix products, arithmetic and copies ran while one was open for 0% of the time, Pallas kernels for 0%

commit v1 on v0

v1 whole, which is shorter than its diff:
```python
import functools

import jax
import jax.numpy as jnp
from jax import lax
from jax.experimental import pallas as pl
from jax.experimental.pallas import tpu as pltpu
from jax.sharding import PartitionSpec as P

SLOTS = 4
GROUP = 4
LOG2E = 1.4426950408889634


def kernel(n, q_hbm, k_hbm, v_hbm, o_ref, qv, kbuf, vbuf, sbuf, parts, stats, q_sem, k_sem, v_sem, part_send, part_recv, stat_send, stat_recv):
    seqs, heads, head = q_hbm.shape
    kv_heads, tokens = k_hbm.shape[1:3]
    rep = heads // kv_heads
    pairs = kv_heads // 2
    rows = 2 * rep
    half = head // 2
    scale = head**-0.5 * LOG2E
    me = lax.axis_index("sp")

    def fetch_k(b, slot):
        return pltpu.make_async_copy(k_hbm.at[b], kbuf.at[slot], k_sem.at[slot])

    def fetch_v(b, slot):
        return pltpu.make_async_copy(v_hbm.at[b], vbuf.at[slot], v_sem.at[slot])

    fetch_q = pltpu.make_async_copy(q_hbm, qv, q_sem)
    fetch_q.start()
    for b in range(SLOTS):
        fetch_k(b, b).start()
        fetch_v(b, b).start()

    barrier = pltpu.get_barrier_semaphore()
    for d in range(1, n):
        pl.semaphore_signal(barrier, inc=1, device_id={"sp": lax.rem(me + d, n)}, device_id_type=pl.DeviceIdType.MESH)

    row = lax.broadcasted_iota(jnp.int32, (rows, head), 0)
    lane = lax.broadcasted_iota(jnp.int32, (rows, head), 1)
    first = row < rep

    def scores(b, slot, into):
        q = qv[b].astype(jnp.float32)
        for p in range(pairs):
            x = q[p * rows : (p + 1) * rows]
            both = jnp.concatenate([jnp.where(first, x, 0.0), jnp.where(first, 0.0, x)], 1).astype(jnp.bfloat16)
            keys = jnp.concatenate([kbuf[slot, 2 * p], kbuf[slot, 2 * p + 1]], 1)
            sbuf[into, p] = lax.dot_general(both, keys, (((1,), (1,)), ((), ())), preferred_element_type=jnp.float32)

    def values(b, slot, source):
        outs = []
        stat = jnp.zeros((rows, head), jnp.float32)
        for p in range(pairs):
            s = sbuf[source, p] * scale
            high = jnp.max(s, 1, keepdims=True)
            w = jnp.exp2(s - high)
            total = jnp.sum(w, 1, keepdims=True)
            vals = jnp.concatenate([vbuf[slot, 2 * p], vbuf[slot, 2 * p + 1]], 1)
            seen = jnp.dot(w.astype(jnp.bfloat16), vals, preferred_element_type=jnp.float32)
            outs.append(jnp.where(first, seen[:, :head], seen[:, head:]))
            stat = jnp.where(lane == p, high, stat)
            stat = jnp.where(lane == half + p, total, stat)
        parts[me, b] = jnp.concatenate(outs, 0).astype(jnp.bfloat16)
        stats[me, b] = stat

    def sends(d, g, start, count):
        to = {"sp": lax.rem(me + d, n)}
        span = pl.ds(start, count)
        return (
            pltpu.make_async_remote_copy(parts.at[me, span], parts.at[me, span], part_send.at[d - 1, g], part_recv.at[d - 1, g], device_id=to, device_id_type=pl.DeviceIdType.MESH),
            pltpu.make_async_remote_copy(stats.at[me, span], stats.at[me, span], stat_send.at[d - 1, g], stat_recv.at[d - 1, g], device_id=to, device_id_type=pl.DeviceIdType.MESH),
        )

    order = [d for d in (2, 1, 3) if d < n]

    def send(g, start, count):
        for d in order:
            for c in sends(d, g, start, count):
                c.start()

    def arrive(g, start, count):
        for d in range(1, n):
            for c in sends(d, g, start, count):
                c.wait_recv()
                c.wait_send()

    def combine(b):
        st = [stats[d, b] for d in range(n)]
        top = functools.reduce(jnp.maximum, st)
        w = [jnp.exp2(s - top) for s in st]
        total = sum(a * pltpu.roll(s, half, 1) for a, s in zip(w, st))
        w = [a / total for a in w]
        x = [parts[d, b].astype(jnp.float32) for d in range(n)]
        outs = []
        for p in range(pairs):
            outs.append(sum(w[d][:, p : p + 1] * x[d][p * rows : (p + 1) * rows] for d in range(n)))
        o_ref[b] = jnp.concatenate(outs, 0).astype(o_ref.dtype)

    fetch_q.wait()
    fetch_k(0, 0).wait()
    scores(0, 0, 0)
    pl.semaphore_wait(barrier, n - 1)

    def step(i, carry):
        slot = lax.rem(i, SLOTS)
        before = lax.rem(i - 1, SLOTS)

        @pl.when(lax.rem(i, GROUP) == 1)
        def _():
            g = i // GROUP

            @pl.when(g >= 1)
            def _():
                send(g - 1, (g - 1) * GROUP, GROUP)

            @pl.when(g >= 2)
            def _():
                arrive(g - 2, (g - 2) * GROUP, GROUP)

                def one(j, c):
                    combine((g - 2) * GROUP + j)
                    return c

                lax.fori_loop(0, GROUP, one, 0)

        fetch_v(i - 1, before).wait()
        fetch_k(i, slot).wait()
        scores(i, slot, lax.rem(i, 2))
        values(i - 1, before, lax.rem(i - 1, 2))

        @pl.when(i + SLOTS < seqs)
        def _():
            fetch_k(i + SLOTS, slot).start()

        @pl.when(i - 1 + SLOTS < seqs)
        def _():
            fetch_v(i - 1 + SLOTS, before).start()

        return carry

    fetch_k_again = fetch_k(SLOTS, 0)
    fetch_k_again.start()
    lax.fori_loop(1, seqs, step, 0)

    groups = seqs // GROUP
    last = seqs - 1
    send(groups - 1, last - GROUP + 1, GROUP - 1)
    fetch_v(last, last % SLOTS).wait()
    values(last, last % SLOTS, last % 2)
    send(groups, last, 1)
    arrive(groups - 2, (groups - 2) * GROUP, GROUP)
    lax.fori_loop(0, GROUP, lambda j, c: (combine((groups - 2) * GROUP + j), c)[1], 0)
    arrive(groups - 1, last - GROUP + 1, GROUP - 1)
    lax.fori_loop(0, GROUP - 1, lambda j, c: (combine(last - GROUP + 1 + j), c)[1], 0)
    arrive(groups, last, 1)
    combine(last)


def solution(mesh):
    n = mesh.shape["sp"]

    def step(q, k, v):
        seqs, heads, head = q.shape
        tokens, kv_heads = k.shape[1:3]
        k, v = (jnp.transpose(a, (0, 2, 1, 3)) for a in (k, v))
        groups = seqs // GROUP + 1
        rows = 2 * heads // kv_heads
        f32, dma = jnp.float32, pltpu.SemaphoreType.DMA
        return pl.pallas_call(
            functools.partial(kernel, n),
            out_shape=jax.ShapeDtypeStruct(q.shape, q.dtype),
            in_specs=[pl.BlockSpec(memory_space=pl.ANY)] * 3,
            out_specs=pl.BlockSpec(memory_space=pltpu.VMEM),
            scratch_shapes=[
                pltpu.VMEM(q.shape, q.dtype),
                pltpu.VMEM((SLOTS, kv_heads, tokens, head), k.dtype),
                pltpu.VMEM((SLOTS, kv_heads, tokens, head), v.dtype),
                pltpu.VMEM((2, kv_heads // 2, rows, tokens), f32),
                pltpu.VMEM((n, seqs, heads, head), jnp.bfloat16),
                pltpu.VMEM((n, seqs, rows, head), f32),
                dma,
                dma((SLOTS,)),
                dma((SLOTS,)),
                dma((n - 1, groups)),
                dma((n - 1, groups)),
                dma((n - 1, groups)),
                dma((n - 1, groups)),
            ],
            compiler_params=pltpu.CompilerParams(collective_id=0, has_side_effects=True, vmem_limit_bytes=60 * 2**20),
        )(q, k, v)

    return jax.shard_map(
        step,
        mesh=mesh,
        in_specs=(P("dp", None, None), P("dp", "sp", None, None), P("dp", "sp", None, None)),
        out_specs=P("dp", None, None),
        check_vma=False,
    )
```

time: 160 us -> 61.2 us (0.38)
  matrix products: 63.1 us -> 0 us
  Pallas kernels: 0 us -> 59.4 us
  waiting for transfers between devices: 55.9 us -> 0 us
  other arithmetic: 17.6 us -> 0 us
  between operations: 13.4 us -> 0.01 us
  local copies, waits for them, and re-layouts: 9.52 us -> 1.73 us
    dot_general x2 -> x0, matrix products: 63.1 us -> none  [einsum(): return jnp.einsum(form, a.astype(jnp.float32), b.astype(jnp.float32))]
    pallas_call x0 -> x1, Pallas kernels: none -> 59.4 us  [step(): pl.pallas_call(functools.partial(kernel, n), out_shape=jax.ShapeDtypeStru...]
    all_gather x1 -> x0, waiting for transfers between devices: 55.8 us -> none  [step(): return together(lax.all_gather(part_of(q, k, v), 'sp')).reshape(q.shape)]
    reduce_sum x3 -> x0, other arithmetic: 9.07 us -> none  [the longest x1 5.32 us: part_of(): jnp.sum(weights, -1, keepdims=True)]
    slice x1 -> x0, other arithmetic: 5.95 us -> none  [together(): seen, total, high = (parts[..., :-2], parts[..., -2:-1], parts[..., -1:])]
    broadcast_in_dim x2 -> x0, local copies, waits for them, and re-layouts: 4.1 us -> none  [the longest x1 2.05 us: part_of(): jnp.sum(weights, -1, keepdims=True)]
    unnamed x5 -> x1, local copies, waits for them, and re-layouts: 4.81 us -> 1.73 us
  transfers between devices with their start and end apart: 1 -> 0, of which waited for: 1 -> 0; matrix products, arithmetic and copies ran while one was open for 0% -> 0% of each run, Pallas kernels for 0% -> 0%
where the time goes in v1:
time: 61.2 us; the launch traced here: 61.1 us
  Pallas kernels  59.4 us (97%)
  local copies, waits for them, and re-layouts  1.73 us (3%)
    pallas_call x1, Pallas kernels, step(): pl.pallas_call(functools.partial(kernel, n), out_shape=jax.ShapeDtypeStru...  59.4 us
    unnamed x1, local copies, waits for them, and re-layouts  1.73 us

profile of v1, /device:TPU:112, one launch (start us, length us, event | category | flops | bytes accessed | tf_op | source)
XLA Modules:
  0.0 61.1 jit_solution(6528473099631669557)
XLA Ops:
  0.0 59.4 %shard_map.37 = bf16[32,40,128]{2,1,0:T(8,128)(2,1)} custom-call(bf16[32,40,128]{2,1,0:T(8,128)(2,1)} %q_hbm.1, bf16[32,10,1024,128]{3,2,1,0:T(8,128)(2,1)} %bitcast.k_hbm, bf16[32,10,1024,128]{3,2,1,0:T(8,128)(2,1)} %bitcast.1.v_hbm), custom_call_target="tpu_custom_call" | custom-call | tf_op jit(solution)/shard_map/pallas_call | solution.py:172
  59.4 1.7 %copy.5 = bf16[32,40,128]{2,1,0:T(8,128)(2,1)} copy(bf16[32,40,128]{2,1,0:T(8,128)(2,1)} %shard_map.37) | data formatting | bytes 655360

commit v2 on v0

v2 whole, which is shorter than its diff:
```python
import functools

import jax
import jax.numpy as jnp
from jax import lax
from jax.experimental import pallas as pl
from jax.experimental.pallas import tpu as pltpu
from jax.sharding import PartitionSpec as P

SLOTS = 4
AHEAD = 6
TILE = 4
LOG2E = 1.4426950408889634
MESH = pl.DeviceIdType.MESH


def kernel(n, q_hbm, k_hbm, v_hbm, o_ref, qv, kbuf, vbuf, sbuf, wbuf, parts, stats, q_sem, k_sem, v_sem, end_sem, part_send, part_recv, stat_send, stat_recv):
    seqs, heads, head = q_hbm.shape
    kv_heads = k_hbm.shape[1]
    rep = heads // kv_heads
    pairs = kv_heads // 2
    rows = 2 * rep
    half = head // 2
    wide = half // TILE
    last = seqs - 1
    tiles = seqs // TILE
    old = tiles // 2
    early = (pairs - 1) * rows
    scale = head**-0.5 * LOG2E
    me = lax.axis_index("sp")
    groups = ((0, old * TILE), (old * TILE, last - TILE + 1), (last - TILE + 1, last))

    def fetch_k(b):
        slot = lax.rem(b, SLOTS)
        return pltpu.make_async_copy(k_hbm.at[b], kbuf.at[slot], k_sem.at[slot])

    def fetch_v(b):
        slot = lax.rem(b, SLOTS)
        return pltpu.make_async_copy(v_hbm.at[b], vbuf.at[slot], v_sem.at[slot])

    def fetch_end(e):
        cut = early // rep
        part = pl.ds(0, cut) if e == 0 else pl.ds(cut, kv_heads - cut)
        return pltpu.make_async_copy(v_hbm.at[last, part], vbuf.at[last % SLOTS, part], end_sem.at[e])

    def fetch_q():
        return pltpu.make_async_copy(q_hbm, qv, q_sem)

    fetch_q().start()
    barrier = pltpu.get_barrier_semaphore()
    for d in range(1, n):
        pl.semaphore_signal(barrier, inc=1, device_id={"sp": lax.rem(me + d, n)}, device_id_type=MESH)
    for b in range(SLOTS):
        fetch_k(b).start()

    first = lax.broadcasted_iota(jnp.int32, (rows, head), 0) < rep
    lane = lax.broadcasted_iota(jnp.int32, (rows, head), 1)

    def scores(b):
        q = qv[b].astype(jnp.float32)
        for p in range(pairs):
            x = q[p * rows : (p + 1) * rows]
            both = jnp.concatenate([jnp.where(first, x, 0.0), jnp.where(first, 0.0, x)], 1).astype(jnp.bfloat16)
            slot = lax.rem(b, SLOTS)
            keys = jnp.concatenate([kbuf[slot, 2 * p], kbuf[slot, 2 * p + 1]], 1)
            sbuf[lax.rem(b, 2), p] = lax.dot_general(both, keys, (((1,), (1,)), ((), ())), preferred_element_type=jnp.float32)

    def weights(b):
        tile = b // TILE
        at = lax.rem(b, TILE) * wide
        stat = stats[me, tile]
        for p in range(pairs):
            s = sbuf[lax.rem(b, 2), p] * scale
            high = jnp.max(s, 1, keepdims=True)
            w = jnp.exp2(s - high)
            total = jnp.sum(w, 1, keepdims=True)
            stat = jnp.where(lane == at + p, high, stat)
            stat = jnp.where(lane == half + at + p, total, stat)
            wbuf[lax.rem(b, AHEAD + 1), p] = w.astype(jnp.bfloat16)
        stats[me, tile] = stat

    def seen(b, p):
        slot = lax.rem(b, SLOTS)
        vals = jnp.concatenate([vbuf[slot, 2 * p], vbuf[slot, 2 * p + 1]], 1)
        out = jnp.dot(wbuf[lax.rem(b, AHEAD + 1), p], vals, preferred_element_type=jnp.float32)
        return jnp.where(first, out[:, :head], out[:, head:])

    def values(b):
        parts[me, b] = jnp.concatenate([seen(b, p) for p in range(pairs)], 0).astype(jnp.bfloat16)

    def to(d):
        return {"sp": lax.rem(me + d, n)}

    peers = sorted(range(1, n), key=lambda d: -min(d, n - d))

    def send(ref, sent, received):
        for d in peers:
            pltpu.make_async_remote_copy(ref, ref, sent.at[0], received, device_id=to(d), device_id_type=MESH).start()

    def send_part(b, g):
        send(parts.at[me, b], part_send, part_recv.at[g])

    def send_stat(t, g):
        send(stats.at[me, t], stat_send, stat_recv.at[g])

    def landed(ref, sem):
        pltpu.make_async_copy(ref, ref, sem).wait()

    others = pl.ds(0, n - 1)

    def shares(t):
        st = [stats[d, t] for d in range(n)]
        top = functools.reduce(jnp.maximum, st)
        w = [jnp.exp2(s - top) for s in st]
        total = sum(a * pltpu.roll(s, half, 1) for a, s in zip(w, st))
        return [a / total for a in w]

    def factors(w, j):
        lanes = [j * wide + p for p in range(pairs)]
        return [[jnp.broadcast_to(a[:, x : x + 1], (rows, head)) for a in w] for x in lanes]

    def mixed(b, ps, f):
        x = [parts[d, b, pl.ds(ps[0] * rows, len(ps) * rows)].astype(jnp.float32) for d in range(n)]
        return jnp.concatenate([sum(f[p][d] * x[d][i * rows : (i + 1) * rows] for d in range(n)) for i, p in enumerate(ps)], 0)

    def combine(t, w, j):
        o_ref[t * TILE + j] = mixed(t * TILE + j, range(pairs), factors(w, j)).astype(o_ref.dtype)

    def combine_tile(t, carry):
        w = shares(t)
        for j in range(TILE):
            combine(t, w, j)
        return carry

    def refill_k(b):
        @pl.when(b < seqs)
        def _():
            fetch_k(b).start()

    def refill_v(b):
        @pl.when((b >= 0) & (b < last))
        def _():
            fetch_v(b).start()

        @pl.when(b == last)
        def _():
            for e in range(2):
                fetch_end(e).start()

    fetch_q().wait()
    fetch_k(0).wait()
    scores(0)
    refill_k(SLOTS)

    def fill(i, carry):
        fetch_k(i).wait()
        weights(i - 1)
        scores(i)
        refill_k(i + SLOTS)
        refill_v(i - AHEAD + SLOTS)
        return carry

    lax.fori_loop(1, AHEAD, fill, 0)
    pl.semaphore_wait(barrier, n - 1)
    send_stat(0, 0)

    def group(b):
        return jnp.where(b < groups[1][0], 0, jnp.where(b < groups[2][0], 1, 2))

    def step(i, carry):
        done = i - AHEAD - 1

        @pl.when(done >= 0)
        def _():
            send_part(done, group(done))

        @pl.when((lax.rem(i, TILE) == 1) & (i >= AHEAD + 1))
        def _():
            t = i // TILE - 1
            send_stat(t, group(t * TILE))

        @pl.when(i == groups[0][1] + AHEAD + TILE)
        def _():
            span = pl.ds(0, groups[0][1])
            landed(parts.at[others, span], part_recv.at[0])
            landed(stats.at[others, pl.ds(0, old)], stat_recv.at[0])
            lax.fori_loop(0, old, combine_tile, 0)

        fetch_k(i).wait()
        fetch_v(i - AHEAD).wait()
        values(i - AHEAD)
        weights(i - 1)
        scores(i)
        refill_k(i + SLOTS)
        refill_v(i - AHEAD + SLOTS)
        return carry

    lax.fori_loop(AHEAD, seqs, step, 0)

    weights(last)
    send_stat(tiles - 1, 2)

    def finish(b, carry):
        fetch_v(b).wait()
        send_part(b - 1, group(b - 1))
        values(b)
        refill_v(b + SLOTS)
        return carry

    lax.fori_loop(last - AHEAD + 1, last, finish, 0)

    fetch_end(0).wait()
    send_part(last - 1, 2)
    parts[me, last, pl.ds(0, early)] = jnp.concatenate([seen(last, p) for p in range(pairs - 1)], 0).astype(jnp.bfloat16)
    fetch_end(1).wait()
    send(parts.at[me, last, pl.ds(0, early)], part_send, part_recv.at[3])
    parts[me, last, pl.ds(early, rows)] = seen(last, pairs - 1).astype(jnp.bfloat16)
    send(parts.at[me, last, pl.ds(early, rows)], part_send, part_recv.at[4])

    landed(parts.at[others, pl.ds(groups[1][0], groups[1][1] - groups[1][0])], part_recv.at[1])
    landed(stats.at[others, pl.ds(old, tiles - 1 - old)], stat_recv.at[1])
    lax.fori_loop(old, tiles - 1, combine_tile, 0)
    landed(stats.at[others, pl.ds(0, 1)], stat_recv.at[2])
    w = shares(tiles - 1)
    landed(parts.at[others, pl.ds(0, TILE - 1)], part_recv.at[2])
    for j in range(TILE - 1):
        combine(tiles - 1, w, j)
    f = factors(w, TILE - 1)
    landed(parts.at[others, last, pl.ds(0, early)], part_recv.at[3])
    o_ref[last, pl.ds(0, early)] = mixed(last, range(pairs - 1), f).astype(o_ref.dtype)
    landed(parts.at[others], part_send.at[0])
    landed(stats.at[others], stat_send.at[0])
    landed(parts.at[others, last, pl.ds(early, rows)], part_recv.at[4])
    o_ref[last, pl.ds(early, rows)] = mixed(last, [pairs - 1], f).astype(o_ref.dtype)


def solution(mesh):
    n = mesh.shape["sp"]

    def step(q, k, v):
        seqs, heads, head = q.shape
        tokens, kv_heads = k.shape[1:3]
        k, v = (jnp.transpose(a, (0, 2, 1, 3)) for a in (k, v))
        pairs, rows = kv_heads // 2, 2 * heads // kv_heads
        f32, bf16, dma = jnp.float32, jnp.bfloat16, pltpu.SemaphoreType.DMA
        return pl.pallas_call(
            functools.partial(kernel, n),
            out_shape=jax.ShapeDtypeStruct(q.shape, q.dtype),
            in_specs=[pl.BlockSpec(memory_space=pl.ANY)] * 3,
            out_specs=pl.BlockSpec(memory_space=pltpu.VMEM),
            scratch_shapes=[
                pltpu.VMEM(q.shape, q.dtype),
                pltpu.VMEM((SLOTS, kv_heads, tokens, head), k.dtype),
                pltpu.VMEM((SLOTS, kv_heads, tokens, head), v.dtype),
                pltpu.VMEM((2, pairs, rows, tokens), f32),
                pltpu.VMEM((AHEAD + 1, pairs, rows, tokens), bf16),
                pltpu.VMEM((n, seqs, heads, head), bf16),
                pltpu.VMEM((n, seqs // TILE, rows, head), f32),
                dma,
                dma((SLOTS,)),
                dma((SLOTS,)),
                dma((2,)),
                dma((1,)),
                dma((5,)),
                dma((1,)),
                dma((3,)),
            ],
            compiler_params=pltpu.CompilerParams(collective_id=0, has_side_effects=True, vmem_limit_bytes=32 * 2**20),
        )(*(pltpu.with_memory_space_constraint(a, pltpu.HBM) for a in (q, k, v)))

    return jax.shard_map(
        step,
        mesh=mesh,
        in_specs=(P("dp", None, None), P("dp", "sp", None, None), P("dp", "sp", None, None)),
        out_specs=P("dp", None, None),
        check_vma=False,
    )
```

time: 160 us -> 56.7 us (0.35)
  matrix products: 63.1 us -> 0 us
  Pallas kernels: 0 us -> 55.9 us
  waiting for transfers between devices: 55.9 us -> 0 us
  other arithmetic: 17.6 us -> 0 us
  between operations: 13.4 us -> 0.01 us
  local copies, waits for them, and re-layouts: 9.52 us -> 0.73 us
    dot_general x2 -> x0, matrix products: 63.1 us -> none  [einsum(): return jnp.einsum(form, a.astype(jnp.float32), b.astype(jnp.float32))]
    pallas_call x0 -> x1, Pallas kernels: none -> 55.9 us  [step(): pl.pallas_call(functools.partial(kernel, n), out_shape=jax.ShapeDtypeStru...]
    all_gather x1 -> x0, waiting for transfers between devices: 55.8 us -> none  [step(): return together(lax.all_gather(part_of(q, k, v), 'sp')).reshape(q.shape)]
    reduce_sum x3 -> x0, other arithmetic: 9.07 us -> none  [the longest x1 5.32 us: part_of(): jnp.sum(weights, -1, keepdims=True)]
    slice x1 -> x0, other arithmetic: 5.95 us -> none  [together(): seen, total, high = (parts[..., :-2], parts[..., -2:-1], parts[..., -1:])]
    broadcast_in_dim x2 -> x0, local copies, waits for them, and re-layouts: 4.1 us -> none  [the longest x1 2.05 us: part_of(): jnp.sum(weights, -1, keepdims=True)]
    unnamed x5 -> x1, local copies, waits for them, and re-layouts: 4.81 us -> 0.73 us
  transfers between devices with their start and end apart: 1 -> 0, of which waited for: 1 -> 0; matrix products, arithmetic and copies ran while one was open for 0% -> 0% of each run, Pallas kernels for 0% -> 0%
where the time goes in v2:
time: 56.7 us; the launch traced here: 56.6 us
  Pallas kernels  55.9 us (99%)
  local copies, waits for them, and re-layouts  0.73 us (1%)
    pallas_call x1, Pallas kernels, step(): pl.pallas_call(functools.partial(kernel, n), out_shape=jax.ShapeDtypeStru...  55.9 us

profile of v2, /device:TPU:112, one launch (start us, length us, event | category | flops | bytes accessed | tf_op | source)
XLA Modules:
  0.0 56.6 jit_solution(11415862680976885836)
XLA Ops:
  0.0 55.9 %shard_map.37 = bf16[32,40,128]{2,1,0:T(8,128)(2,1)S(1)} custom-call(bf16[32,40,128]{2,1,0:T(8,128)(2,1)} %q_hbm.1, bf16[32,10,1024,128]{3,2,1,0:T(8,128)(2,1)} %bitcast.k_hbm, bf16[32,10,1024,128]{3,2,1,0:T(8,128)(2,1)} %bitcast.1.v_hbm), custom_call_target="tpu_custom_call" | custom-call | tf_op jit(solution)/shard_map/pallas_call | solution.py:246
  55.9 0.7 %copy.5 = bf16[32,40,128]{2,1,0:T(8,128)(2,1)} copy(bf16[32,40,128]{2,1,0:T(8,128)(2,1)S(1)} %shard_map.37) | data formatting | bytes 655360

commit v3 on v2

v3 whole, which is shorter than its diff:
```python
import functools

import jax
import jax.numpy as jnp
from jax import lax
from jax.experimental import pallas as pl
from jax.experimental.pallas import tpu as pltpu
from jax.sharding import PartitionSpec as P

SLOTS = 4
AHEAD = 6
TILE = 4
LOG2E = 1.4426950408889634
MESH = pl.DeviceIdType.MESH
dma = pltpu.SemaphoreType.DMA


def kernel(n, q_hbm, k_hbm, v_hbm, o_ref, qv, kbuf, vbuf, sbuf, wbuf, parts, stats, part_send, part_recv, stat_send, stat_recv):
    seqs, heads, head = q_hbm.shape
    kv_heads = k_hbm.shape[1]
    rep = heads // kv_heads
    pairs = kv_heads // 2
    rows = 2 * rep
    half = head // 2
    wide = half // TILE
    last = seqs - 1
    tiles = seqs // TILE
    old = tiles // 2
    ahead = pairs - 2
    early = ahead * rows
    scale = head**-0.5 * LOG2E
    me = lax.axis_index("sp")
    groups = ((0, old * TILE), (old * TILE, last - TILE + 1), (last - TILE + 1, last))

    first = lax.broadcasted_iota(jnp.int32, (rows, head), 0) < rep
    lane = lax.broadcasted_iota(jnp.int32, (rows, head), 1)

    def scores(b):
        q = qv[b].astype(jnp.float32)
        for p in range(pairs):
            x = q[p * rows : (p + 1) * rows]
            both = jnp.concatenate([jnp.where(first, x, 0.0), jnp.where(first, 0.0, x)], 1).astype(jnp.bfloat16)
            slot = lax.rem(b, SLOTS)
            keys = jnp.concatenate([kbuf[slot, 2 * p], kbuf[slot, 2 * p + 1]], 1)
            sbuf[lax.rem(b, 2), p] = lax.dot_general(both, keys, (((1,), (1,)), ((), ())), preferred_element_type=jnp.float32)

    def weights(b):
        tile = b // TILE
        at = lax.rem(b, TILE) * wide
        stat = stats[me, tile]
        for p in range(pairs):
            s = sbuf[lax.rem(b, 2), p] * scale
            high = jnp.max(s, 1, keepdims=True)
            w = jnp.exp2(s - high)
            total = jnp.sum(w, 1, keepdims=True)
            stat = jnp.where(lane == at + p, high, stat)
            stat = jnp.where(lane == half + at + p, total, stat)
            wbuf[lax.rem(b, AHEAD + 1), p] = w.astype(jnp.bfloat16)
        stats[me, tile] = stat

    def seen(b, p):
        slot = lax.rem(b, SLOTS)
        vals = jnp.concatenate([vbuf[slot, 2 * p], vbuf[slot, 2 * p + 1]], 1)
        out = jnp.dot(wbuf[lax.rem(b, AHEAD + 1), p], vals, preferred_element_type=jnp.float32)
        return jnp.where(first, out[:, :head], out[:, head:])

    def values(b):
        parts[me, b] = jnp.concatenate([seen(b, p) for p in range(pairs)], 0).astype(jnp.bfloat16)

    def to(d):
        return {"sp": lax.rem(me + d, n)}

    peers = sorted(range(1, n), key=lambda d: -min(d, n - d))

    def send(ref, sent, received):
        for d in peers:
            pltpu.make_async_remote_copy(ref, ref, sent.at[0], received, device_id=to(d), device_id_type=MESH).start()

    def send_part(b, g):
        send(parts.at[me, b], part_send, part_recv.at[g])

    def send_stat(t, g):
        send(stats.at[me, t], stat_send, stat_recv.at[g])

    def landed(ref, sem):
        pltpu.make_async_copy(ref, ref, sem).wait()

    others = pl.ds(0, n - 1)

    def shares(t):
        st = [stats[d, t] for d in range(n)]
        top = functools.reduce(jnp.maximum, st)
        w = [jnp.exp2(s - top) for s in st]
        total = sum(a * pltpu.roll(s, half, 1) for a, s in zip(w, st))
        return [a / total for a in w]

    def factors(w, j):
        lanes = [j * wide + p for p in range(pairs)]
        return [[jnp.broadcast_to(a[:, x : x + 1], (rows, head)) for a in w] for x in lanes]

    def mixed(b, ps, f):
        x = [parts[d, b, pl.ds(ps[0] * rows, len(ps) * rows)].astype(jnp.float32) for d in range(n)]
        return jnp.concatenate([sum(f[p][d] * x[d][i * rows : (i + 1) * rows] for d in range(n)) for i, p in enumerate(ps)], 0)

    def combine(t, w, j):
        o_ref[t * TILE + j] = mixed(t * TILE + j, range(pairs), factors(w, j)).astype(o_ref.dtype)

    def combine_tile(t, carry):
        w = shares(t)
        for j in range(TILE):
            combine(t, w, j)
        return carry

    @functools.partial(pl.run_scoped, q_sem=dma, k_sem=dma((SLOTS,)), v_sem=dma((SLOTS,)), end_sem=dma((2,)))
    def _(q_sem, k_sem, v_sem, end_sem):
        def fetch_k(b):
            slot = lax.rem(b, SLOTS)
            return pltpu.make_async_copy(k_hbm.at[b], kbuf.at[slot], k_sem.at[slot])

        def fetch_v(b):
            slot = lax.rem(b, SLOTS)
            return pltpu.make_async_copy(v_hbm.at[b], vbuf.at[slot], v_sem.at[slot])

        def fetch_end(e):
            cut = early // rep
            part = pl.ds(0, cut) if e == 0 else pl.ds(cut, kv_heads - cut)
            return pltpu.make_async_copy(v_hbm.at[last, part], vbuf.at[last % SLOTS, part], end_sem.at[e])

        def fetch_q():
            return pltpu.make_async_copy(q_hbm, qv, q_sem)

        fetch_q().start()
        barrier = pltpu.get_barrier_semaphore()
        for d in range(1, n):
            pl.semaphore_signal(barrier, inc=1, device_id={"sp": lax.rem(me + d, n)}, device_id_type=MESH)
        for b in range(SLOTS):
            fetch_k(b).start()

        def refill_k(b):
            @pl.when(b < seqs)
            def _():
                fetch_k(b).start()

        def refill_v(b):
            @pl.when((b >= 0) & (b < last))
            def _():
                fetch_v(b).start()

            @pl.when(b == last)
            def _():
                for e in range(2):
                    fetch_end(e).start()

        fetch_q().wait()
        fetch_k(0).wait()
        scores(0)
        refill_k(SLOTS)

        def fill(i, carry):
            fetch_k(i).wait()
            weights(i - 1)
            scores(i)
            refill_k(i + SLOTS)
            refill_v(i - AHEAD + SLOTS)
            return carry

        lax.fori_loop(1, AHEAD, fill, 0)
        pl.semaphore_wait(barrier, n - 1)
        send_stat(0, 0)

        def group(b):
            return jnp.where(b < groups[1][0], 0, jnp.where(b < groups[2][0], 1, 2))

        def step(i, carry):
            done = i - AHEAD - 1

            @pl.when(done >= 0)
            def _():
                send_part(done, group(done))

            @pl.when((lax.rem(i, TILE) == 1) & (i >= AHEAD + 1))
            def _():
                t = i // TILE - 1
                send_stat(t, jnp.minimum(group(t * TILE), 1))

            @pl.when(i == groups[0][1] + AHEAD + TILE)
            def _():
                span = pl.ds(0, groups[0][1])
                landed(parts.at[others, span], part_recv.at[0])
                landed(stats.at[others, pl.ds(0, old)], stat_recv.at[0])
                lax.fori_loop(0, old, combine_tile, 0)

            fetch_k(i).wait()
            fetch_v(i - AHEAD).wait()
            values(i - AHEAD)
            weights(i - 1)
            scores(i)
            refill_k(i + SLOTS)
            refill_v(i - AHEAD + SLOTS)
            return carry

        lax.fori_loop(AHEAD, seqs, step, 0)

        weights(last)
        send_stat(tiles - 1, 1)

        def finish(b, carry):
            fetch_v(b).wait()
            send_part(b - 1, group(b - 1))
            values(b)
            refill_v(b + SLOTS)
            return carry

        lax.fori_loop(last - AHEAD + 1, last, finish, 0)

        fetch_end(0).wait()
        send_part(last - 1, 2)
        outs = [seen(last, p) for p in range(ahead)]
        fetch_end(1).wait()
        parts[me, last, pl.ds(0, early)] = jnp.concatenate(outs, 0).astype(jnp.bfloat16)
        outs = [seen(last, p) for p in range(ahead, pairs)]
        parts[me, last, pl.ds(early, heads - early)] = jnp.concatenate(outs, 0).astype(jnp.bfloat16)
        send(parts.at[me, last], part_send, part_recv.at[3])

    landed(parts.at[others, pl.ds(groups[1][0], groups[1][1] - groups[1][0])], part_recv.at[1])
    landed(stats.at[others, pl.ds(old, tiles - old)], stat_recv.at[1])
    lax.fori_loop(old, tiles - 1, combine_tile, 0)
    w = shares(tiles - 1)
    landed(parts.at[others, pl.ds(0, TILE - 1)], part_recv.at[2])
    for j in range(TILE - 1):
        combine(tiles - 1, w, j)
    f = factors(w, TILE - 1)
    landed(parts.at[others], part_send.at[0])
    landed(stats.at[others], stat_send.at[0])
    landed(parts.at[others, last], part_recv.at[3])
    o_ref[last] = mixed(last, range(pairs), f).astype(o_ref.dtype)


def solution(mesh):
    n = mesh.shape["sp"]

    def step(q, k, v):
        seqs, heads, head = q.shape
        tokens, kv_heads = k.shape[1:3]
        k, v = (jnp.transpose(a, (0, 2, 1, 3)) for a in (k, v))
        pairs, rows = kv_heads // 2, 2 * heads // kv_heads
        f32, bf16 = jnp.float32, jnp.bfloat16
        return pl.pallas_call(
            functools.partial(kernel, n),
            out_shape=jax.ShapeDtypeStruct(q.shape, q.dtype),
            in_specs=[pl.BlockSpec(memory_space=pl.ANY)] * 3,
            out_specs=pl.BlockSpec(memory_space=pltpu.VMEM),
            scratch_shapes=[
                pltpu.VMEM(q.shape, q.dtype),
                pltpu.VMEM((SLOTS, kv_heads, tokens, head), k.dtype),
                pltpu.VMEM((SLOTS, kv_heads, tokens, head), v.dtype),
                pltpu.VMEM((2, pairs, rows, tokens), f32),
                pltpu.VMEM((AHEAD + 1, pairs, rows, tokens), bf16),
                pltpu.VMEM((n, seqs, heads, head), bf16),
                pltpu.VMEM((n, seqs // TILE, rows, head), f32),
                dma((1,)),
                dma((4,)),
                dma((1,)),
                dma((2,)),
            ],
            compiler_params=pltpu.CompilerParams(collective_id=0, has_side_effects=True, vmem_limit_bytes=32 * 2**20),
        )(*(pltpu.with_memory_space_constraint(a, pltpu.HBM) for a in (q, k, v)))

    return jax.shard_map(
        step,
        mesh=mesh,
        in_specs=(P("dp", None, None), P("dp", "sp", None, None), P("dp", "sp", None, None)),
        out_specs=P("dp", None, None),
        check_vma=False,
    )
```

time: 56.7 us -> 56.4 us (level)
  no operation moved by 1% of the time
where the time goes in v3:
time: 56.4 us; the launch traced here: 56.3 us
  Pallas kernels  55.6 us (99%)
  local copies, waits for them, and re-layouts  0.73 us (1%)
    pallas_call x1, Pallas kernels, step(): pl.pallas_call(functools.partial(kernel, n), out_shape=jax.ShapeDtypeStru...  55.6 us

profile of v3, /device:TPU:112, one launch (start us, length us, event | category | flops | bytes accessed | tf_op | source)
XLA Modules:
  0.0 56.3 jit_solution(15689920092939657717)
XLA Ops:
  0.0 55.6 %shard_map.37 = bf16[32,40,128]{2,1,0:T(8,128)(2,1)S(1)} custom-call(bf16[32,40,128]{2,1,0:T(8,128)(2,1)} %q_hbm.1, bf16[32,10,1024,128]{3,2,1,0:T(8,128)(2,1)} %bitcast.k_hbm, bf16[32,10,1024,128]{3,2,1,0:T(8,128)(2,1)} %bitcast.1.v_hbm), custom_call_target="tpu_custom_call" | custom-call | tf_op jit(solution)/shard_map/pallas_call | solution.py:248
  55.6 0.7 %copy.5 = bf16[32,40,128]{2,1,0:T(8,128)(2,1)} copy(bf16[32,40,128]{2,1,0:T(8,128)(2,1)S(1)} %shard_map.37) | data formatting | bytes 655360

commit v4 on v3

--- a/solution.py
+++ b/solution.py
@@ -216,11 +216,12 @@
         fetch_end(0).wait()
         send_part(last - 1, 2)
         outs = [seen(last, p) for p in range(ahead)]
+        parts[me, last, pl.ds(0, early)] = jnp.concatenate(outs, 0).astype(jnp.bfloat16)
+        send(parts.at[me, last, pl.ds(0, early)], part_send, part_recv.at[3])
         fetch_end(1).wait()
-        parts[me, last, pl.ds(0, early)] = jnp.concatenate(outs, 0).astype(jnp.bfloat16)
         outs = [seen(last, p) for p in range(ahead, pairs)]
         parts[me, last, pl.ds(early, heads - early)] = jnp.concatenate(outs, 0).astype(jnp.bfloat16)
-        send(parts.at[me, last], part_send, part_recv.at[3])
+        send(parts.at[me, last, pl.ds(early, heads - early)], part_send, part_recv.at[4])
 
     landed(parts.at[others, pl.ds(groups[1][0], groups[1][1] - groups[1][0])], part_recv.at[1])
     landed(stats.at[others, pl.ds(old, tiles - old)], stat_recv.at[1])
@@ -230,10 +231,12 @@
     for j in range(TILE - 1):
         combine(tiles - 1, w, j)
     f = factors(w, TILE - 1)
+    landed(parts.at[others, last, pl.ds(0, early)], part_recv.at[3])
+    o_ref[last, pl.ds(0, early)] = mixed(last, range(ahead), f).astype(o_ref.dtype)
     landed(parts.at[others], part_send.at[0])
     landed(stats.at[others], stat_send.at[0])
-    landed(parts.at[others, last], part_recv.at[3])
-    o_ref[last] = mixed(last, range(pairs), f).astype(o_ref.dtype)
+    landed(parts.at[others, last, pl.ds(early, heads - early)], part_recv.at[4])
+    o_ref[last, pl.ds(early, heads - early)] = mixed(last, range(ahead, pairs), f).astype(o_ref.dtype)
 
 
 def solution(mesh):
@@ -259,7 +262,7 @@
                 pltpu.VMEM((n, seqs, heads, head), bf16),
                 pltpu.VMEM((n, seqs // TILE, rows, head), f32),
                 dma((1,)),
-                dma((4,)),
+                dma((5,)),
                 dma((1,)),
                 dma((2,)),
             ],

time: 56.4 us -> 56.3 us (level)
  no operation moved by 1% of the time
where the time goes in v4:
time: 56.3 us; the launch traced here: 56.2 us
  Pallas kernels  55.5 us (99%)
  local copies, waits for them, and re-layouts  0.73 us (1%)
    pallas_call x1, Pallas kernels, step(): pl.pallas_call(functools.partial(kernel, n), out_shape=jax.ShapeDtypeStru...  55.5 us

profile of v4, /device:TPU:112, one launch (start us, length us, event | category | flops | bytes accessed | tf_op | source)
XLA Modules:
  0.0 56.2 jit_solution(6564306917007266258)
XLA Ops:
  0.0 55.5 %shard_map.37 = bf16[32,40,128]{2,1,0:T(8,128)(2,1)S(1)} custom-call(bf16[32,40,128]{2,1,0:T(8,128)(2,1)} %q_hbm.1, bf16[32,10,1024,128]{3,2,1,0:T(8,128)(2,1)} %bitcast.k_hbm, bf16[32,10,1024,128]{3,2,1,0:T(8,128)(2,1)} %bitcast.1.v_hbm), custom_call_target="tpu_custom_call" | custom-call | tf_op jit(solution)/shard_map/pallas_call | solution.py:251
  55.5 0.7 %copy.5 = bf16[32,40,128]{2,1,0:T(8,128)(2,1)} copy(bf16[32,40,128]{2,1,0:T(8,128)(2,1)S(1)} %shard_map.37) | data formatting | bytes 655360

commit v5 on v4

--- a/solution.py
+++ b/solution.py
@@ -15,7 +15,7 @@
 dma = pltpu.SemaphoreType.DMA
 
 
-def kernel(n, q_hbm, k_hbm, v_hbm, o_ref, qv, kbuf, vbuf, sbuf, wbuf, parts, stats, part_send, part_recv, stat_send, stat_recv):
+def kernel(n, q_hbm, k_hbm, v_hbm, o_ref, qv, kbuf, vbuf, sbuf, wbuf, parts, stats, part_recv, stat_recv):
     seqs, heads, head = q_hbm.shape
     kv_heads = k_hbm.shape[1]
     rep = heads // kv_heads
@@ -76,12 +76,6 @@
         for d in peers:
             pltpu.make_async_remote_copy(ref, ref, sent.at[0], received, device_id=to(d), device_id_type=MESH).start()
 
-    def send_part(b, g):
-        send(parts.at[me, b], part_send, part_recv.at[g])
-
-    def send_stat(t, g):
-        send(stats.at[me, t], stat_send, stat_recv.at[g])
-
     def landed(ref, sem):
         pltpu.make_async_copy(ref, ref, sem).wait()
 
@@ -111,8 +105,14 @@
             combine(t, w, j)
         return carry
 
-    @functools.partial(pl.run_scoped, q_sem=dma, k_sem=dma((SLOTS,)), v_sem=dma((SLOTS,)), end_sem=dma((2,)))
-    def _(q_sem, k_sem, v_sem, end_sem):
+    @functools.partial(pl.run_scoped, part_send=dma((1,)), stat_send=dma((1,)), q_sem=dma, k_sem=dma((SLOTS,)), v_sem=dma((SLOTS,)), end_sem=dma((2,)))
+    def _(part_send, stat_send, q_sem, k_sem, v_sem, end_sem):
+        def send_part(b, g):
+            send(parts.at[me, b], part_send, part_recv.at[g])
+
+        def send_stat(t, g):
+            send(stats.at[me, t], stat_send, stat_recv.at[g])
+
         def fetch_k(b):
             slot = lax.rem(b, SLOTS)
             return pltpu.make_async_copy(k_hbm.at[b], kbuf.at[slot], k_sem.at[slot])
@@ -222,6 +222,8 @@
         outs = [seen(last, p) for p in range(ahead, pairs)]
         parts[me, last, pl.ds(early, heads - early)] = jnp.concatenate(outs, 0).astype(jnp.bfloat16)
         send(parts.at[me, last, pl.ds(early, heads - early)], part_send, part_recv.at[4])
+        landed(parts.at[others], part_send.at[0])
+        landed(stats.at[others], stat_send.at[0])
 
     landed(parts.at[others, pl.ds(groups[1][0], groups[1][1] - groups[1][0])], part_recv.at[1])
     landed(stats.at[others, pl.ds(old, tiles - old)], stat_recv.at[1])
@@ -233,8 +235,6 @@
     f = factors(w, TILE - 1)
     landed(parts.at[others, last, pl.ds(0, early)], part_recv.at[3])
     o_ref[last, pl.ds(0, early)] = mixed(last, range(ahead), f).astype(o_ref.dtype)
-    landed(parts.at[others], part_send.at[0])
-    landed(stats.at[others], stat_send.at[0])
     landed(parts.at[others, last, pl.ds(early, heads - early)], part_recv.at[4])
     o_ref[last, pl.ds(early, heads - early)] = mixed(last, range(ahead, pairs), f).astype(o_ref.dtype)
 
@@ -261,9 +261,7 @@
                 pltpu.VMEM((AHEAD + 1, pairs, rows, tokens), bf16),
                 pltpu.VMEM((n, seqs, heads, head), bf16),
                 pltpu.VMEM((n, seqs // TILE, rows, head), f32),
-                dma((1,)),
                 dma((5,)),
-                dma((1,)),
                 dma((2,)),
             ],
             compiler_params=pltpu.CompilerParams(collective_id=0, has_side_effects=True, vmem_limit_bytes=32 * 2**20),

time: 56.3 us -> 56.3 us (level)
  no operation moved by 1% of the time
where the time goes in v5:
time: 56.3 us; the launch traced here: 56.2 us
  Pallas kernels  55.5 us (99%)
  local copies, waits for them, and re-layouts  0.73 us (1%)
    pallas_call x1, Pallas kernels, step(): pl.pallas_call(functools.partial(kernel, n), out_shape=jax.ShapeDtypeStru...  55.5 us

profile of v5, /device:TPU:112, one launch (start us, length us, event | category | flops | bytes accessed | tf_op | source)
XLA Modules:
  0.0 56.2 jit_solution(5400234204454415273)
XLA Ops:
  0.0 55.5 %shard_map.37 = bf16[32,40,128]{2,1,0:T(8,128)(2,1)S(1)} custom-call(bf16[32,40,128]{2,1,0:T(8,128)(2,1)} %q_hbm.1, bf16[32,10,1024,128]{3,2,1,0:T(8,128)(2,1)} %bitcast.k_hbm, bf16[32,10,1024,128]{3,2,1,0:T(8,128)(2,1)} %bitcast.1.v_hbm), custom_call_target="tpu_custom_call" | custom-call | tf_op jit(solution)/shard_map/pallas_call | solution.py:251
  55.5 0.7 %copy.5 = bf16[32,40,128]{2,1,0:T(8,128)(2,1)} copy(bf16[32,40,128]{2,1,0:T(8,128)(2,1)S(1)} %shard_map.37) | data formatting | bytes 655360
